TPU v7x, 32 devices: a whole 2x2x4 slice. The times are simulated.
32 devices in a mesh: cp: 8 (over y, x, core), tp: 4 (over z).
Axes of the slice: x: 2, y: 2, z: 4, core: 2. Of those that a mesh axis runs over, the one named last changes fastest.
Arguments:
- hidden: bfloat16 [2048, 4096], P('cp', 'tp'), may hold values from -120 to 120
- query_weight: bfloat16 [4096, 4096], P(None, 'tp'), may hold values from -0.1875 to 0.1875
- key_matrix: bfloat16 [4096, 512], P(None, 'tp'), may hold values from -0.09375 to 0.09375
- value_matrix: bfloat16 [4096, 512], P(None, 'tp'), may hold values from -0.09375 to 0.09375
- output_weight: bfloat16 [4096, 4096], P('tp'), may hold values from -0.1875 to 0.1875
- document_bounds: int32 [9], replicated, may hold values from 0 to 2048, as said below
- block_owner: int32 [16], replicated, may hold values from 0 to 7, as said below
Outputs:
- attended: bfloat16 [2048, 4096], P('cp', 'tp')
Inputs may be any that keep to these rules, and one draw needn't show every extreme that they name: document_bounds[0] = 0, document_bounds[8] = 2048, strictly rising; document i holds the tokens from document_bounds[i] to document_bounds[i + 1] - 1. `block_owner`: every index of cp is named by exactly 2 blocks.
All inputs are finite; a program needn't handle non-finite values.
Results may differ from a plain program's by a relative error of at most 0.012.
The roundings to bfloat16 on the way count: a program that leaves them out, or rounds other values in their place, can miss the bound.
Values may be sent and summed in bfloat16 or wider, within the bound.
A program may use at most 128 MiB of HBM per device.

v0:
```python
import math

import jax
import jax.numpy as jnp
from jax import lax
from jax.sharding import PartitionSpec as P

HEAD_WIDTH = 128
BLOCK = 128


rope_theta = 500000.0
rope_factor = 8.0
rope_context = 8192.0
masked_score = -1e30


def rope_inverse(head_size):
    halves = jnp.arange(head_size // 2, dtype=jnp.float32)
    inverse = 1.0 / rope_theta ** (2.0 * halves / head_size)
    wavelength = 2.0 * math.pi / inverse
    smooth = (rope_context / wavelength - 1.0) / 3.0
    blended = (1.0 - smooth) * inverse / rope_factor + smooth * inverse
    longer = jnp.where(wavelength > rope_context, inverse / rope_factor, blended)
    return jnp.where(wavelength < rope_context / 4.0, inverse, longer)


def document_of(tokens, bounds):
    inner_bounds = bounds[1:-1]
    return jnp.sum((tokens[:, None] >= inner_bounds[None, :]).astype(jnp.int32), axis=1)


def position_of(tokens, bounds):
    starts = bounds[:-1]
    document_start = jnp.max(
        jnp.where(starts[None, :] <= tokens[:, None], starts[None, :], 0), axis=1
    )
    return tokens - document_start


def rotate(raw_rows, tokens, bounds, head_size):
    row_count = raw_rows.shape[0]
    head_count = raw_rows.shape[1] // head_size
    angles = (
        position_of(tokens, bounds).astype(jnp.float32)[:, None] * rope_inverse(head_size)[None, :]
    )
    cosine = jnp.cos(angles)[:, None, :]
    sine_table = jnp.sin(angles)[:, None, :]
    heads_view = raw_rows.reshape(row_count, head_count, head_size)
    front_half = heads_view[:, :, : head_size // 2]
    back_half = heads_view[:, :, head_size // 2 :]
    turned = jnp.concatenate(
        [
            front_half * cosine - back_half * sine_table,
            back_half * cosine + front_half * sine_table,
        ],
        axis=2,
    )
    return turned.reshape(row_count, head_count * head_size).astype(jnp.bfloat16)


def owner_order(block_owner, per_device):
    block_count = block_owner.shape[0]
    blocks = jnp.arange(block_count, dtype=jnp.int32)
    same_owner = block_owner[:, None] == block_owner[None, :]
    earlier = blocks[None, :] < blocks[:, None]
    owner_rank = jnp.sum((same_owner & earlier).astype(jnp.int32), axis=1)
    target = block_owner * per_device + owner_rank
    return jnp.sum(jnp.where(target[None, :] == blocks[:, None], blocks[None, :], 0), axis=1)


def relayout(local_rows, block_order):
    cp_size = lax.axis_size("cp")
    row_count, row_width = local_rows.shape
    per_device = row_count // BLOCK
    portion = BLOCK // cp_size
    pieces = local_rows.reshape(per_device, cp_size, portion * row_width)
    spread = lax.all_to_all(pieces, "cp", split_axis=1, concat_axis=0, tiled=True)
    spread = spread.reshape(per_device * cp_size, portion * row_width)
    wanted = block_order.reshape(cp_size, per_device).T.reshape(-1)
    outgoing = jnp.take(spread, wanted, axis=0).reshape(per_device, cp_size, portion * row_width)
    arrived = lax.all_to_all(outgoing, "cp", split_axis=1, concat_axis=1, tiled=True)
    return arrived.reshape(row_count, row_width)


def project(local_rows, query_weight, key_matrix, value_matrix):
    weight_list = (query_weight, key_matrix, value_matrix)
    portion = lax.all_gather(local_rows, "tp", axis=1, tiled=True)
    return tuple(
        (jnp.dot(portion, weight, preferred_element_type=jnp.float32) for weight in weight_list)
    )


def attend(queries, query_tokens, key_rows, value_rows, key_tokens, bounds, head_size, kv_heads):
    row_count = queries.shape[0]
    query_group_width = queries.shape[1] // (kv_heads * head_size)
    grouped = queries.reshape(row_count, kv_heads, query_group_width, head_size).transpose(
        1, 2, 0, 3
    )
    grouped = grouped.reshape(kv_heads, query_group_width * row_count, head_size)
    query_documents = document_of(query_tokens, bounds)
    score_scale = 1.0 / math.sqrt(head_size)

    def update(flash_state, key_block, value_block, token_block):
        block_rows = key_block.shape[0]
        key_documents = document_of(token_block, bounds)
        allowed = (query_documents[:, None] == key_documents[None, :]) & (
            token_block[None, :] <= query_tokens[:, None]
        )
        running_max, running_sum, running_out = flash_state
        per_head_keys = key_block.reshape(block_rows, kv_heads, head_size).transpose(1, 0, 2)
        per_head_values = value_block.reshape(block_rows, kv_heads, head_size).transpose(1, 0, 2)
        scores = (
            jnp.einsum("khd,ksd->khs", grouped, per_head_keys, preferred_element_type=jnp.float32)
            * score_scale
        )
        wide_mask = jnp.tile(allowed, (query_group_width, 1))[None, :, :]
        scores = jnp.where(wide_mask, scores, masked_score)
        new_max = jnp.maximum(running_max, jnp.max(scores, axis=2))
        weights = jnp.where(wide_mask, jnp.exp(scores - new_max[:, :, None]), 0.0)
        factor = jnp.exp(running_max - new_max)
        new_sum = running_sum * factor + jnp.sum(weights, axis=2)
        new_out = running_out * factor[:, :, None] + jnp.einsum(
            "khs,ksd->khd",
            weights.astype(jnp.bfloat16),
            per_head_values,
            preferred_element_type=jnp.float32,
        )
        return (new_max, new_sum, new_out)

    initial = (
        jnp.full((kv_heads, query_group_width * row_count), masked_score, jnp.float32),
        jnp.zeros((kv_heads, query_group_width * row_count), jnp.float32),
        jnp.zeros((kv_heads, query_group_width * row_count, head_size), jnp.float32),
    )
    key_part = lax.all_gather(key_rows, "cp", axis=0, tiled=True)
    value_part = lax.all_gather(value_rows, "cp", axis=0, tiled=True)
    token_part = lax.all_gather(key_tokens, "cp", axis=0, tiled=True)
    part_rows = key_part.shape[0]
    block_rows = math.gcd(part_rows, 512)

    def one_block(block_index, inner_state):
        first_row = block_index * block_rows
        return update(
            inner_state,
            lax.dynamic_slice_in_dim(key_part, first_row, block_rows, 0),
            lax.dynamic_slice_in_dim(value_part, first_row, block_rows, 0),
            lax.dynamic_slice_in_dim(token_part, first_row, block_rows, 0),
        )

    final_max, final_sum, final_out = lax.fori_loop(0, part_rows // block_rows, one_block, initial)
    normalized = final_out / final_sum[:, :, None]
    merged = normalized.reshape(kv_heads, query_group_width, row_count, head_size).transpose(
        2, 0, 1, 3
    )
    return merged.reshape(row_count, kv_heads * query_group_width * head_size).astype(jnp.bfloat16)


def output_rows(heads_out, output_weight):
    head_terms = jnp.dot(heads_out, output_weight, preferred_element_type=jnp.float32)
    return lax.psum_scatter(head_terms.astype(jnp.bfloat16), "tp", scatter_dimension=1, tiled=True)


def local(
    hidden, query_weight, key_matrix, value_matrix, output_weight, document_bounds, block_owner
):
    cp_index = lax.axis_index("cp")
    row_count = hidden.shape[0]
    per_device = row_count // BLOCK
    block_order = owner_order(block_owner, per_device)
    own_blocks = lax.dynamic_slice_in_dim(block_order, cp_index * per_device, per_device, 0)
    new_tokens = (
        own_blocks[:, None] * BLOCK + jnp.arange(BLOCK, dtype=jnp.int32)[None, :]
    ).reshape(-1)
    kv_heads = key_matrix.shape[1] // HEAD_WIDTH
    moved = relayout(hidden, block_order)
    query_raw, key_raw, value_raw = project(moved, query_weight, key_matrix, value_matrix)
    queries = rotate(query_raw, new_tokens, document_bounds, HEAD_WIDTH)
    key_rows = rotate(key_raw, new_tokens, document_bounds, HEAD_WIDTH)
    value_rows = value_raw.astype(jnp.bfloat16)
    heads_out = attend(
        queries, new_tokens, key_rows, value_rows, new_tokens, document_bounds, HEAD_WIDTH, kv_heads
    )
    return output_rows(heads_out, output_weight)


def solution(mesh):
    placed = (P("cp", "tp"), P(None, "tp"), P(None, "tp"), P(None, "tp"), P("tp", None), P(), P())
    return jax.shard_map(
        local, mesh=mesh, in_specs=placed, out_specs=P("cp", "tp"), check_vma=False
    )
```

profile of v0, /device:TPU:0, one launch (start us, length us, event | category | flops | bytes accessed | tf_op | source)
XLA Modules:
  0.0 201.7 jit_solution(1744247314047454510)
XLA Ops:
  6.5 1.4 reshape.365
  7.9 1.3 copy.37
  9.2 5.2 %all-to-all-start = ((bf16[2,8,16384]{2,0,1:T(2,128)(2,1)}), bf16[2,8,16384]{2,0,1:T(2,128)(2,1)S(1)}, u32[]{:S(2)}, u32[]{:S(2)}) async-start(bf16[2,8,16384]{2,0,1:T(2,128)(2,1)} %copy.37), calls=%async_computation | async-start | bytes 1048576 | tf_op jit(solution)/shard_map/all_to_all | solution.py:78
  14.5 0.9 convert_reduce_fusion.2
  15.4 0.7 multiply_add_fusion
  16.5 7.7 %all-to-all-done = bf16[2,8,16384]{2,0,1:T(2,128)(2,1)S(1)} async-done(((bf16[2,8,16384]{2,0,1:T(2,128)(2,1)}), bf16[2,8,16384]{2,0,1:T(2,128)(2,1)S(1)}, u32[]{:S(2)}, u32[]{:S(2)}) %all-to-all-start) | async-done | bytes 524320 | tf_op jit(solution)/shard_map/all_to_all | solution.py:78
  24.4 0.9 gather_fusion
  25.3 0.9 broadcast_select_fusion.2
  26.2 12.1 %all_to_all.20 = bf16[2,8,16384]{2,0,1:T(2,128)(2,1)S(1)} all-to-all(bf16[2,8,16384]{2,0,1:T(2,128)(2,1)S(1)} %broadcast_select_fusion.2), channel_id=1, replica_groups=mesh['cp'=8,'tp'=4] {'cp'}, dimensions={1} | all-to-all | bytes 1048576 | tf_op jit(solution)/shard_map/all_to_all | solution.py:82
  38.3 0.3 copy.40
  38.6 1.0 reshape.368
  40.0 8.0 %all-gather.1 = s32[8,1,256]{2,1,0:T(1,128)S(1)} all-gather(s32[1,1,256]{2,1,0:T(1,128)S(1)} %bitcast.115), channel_id=1, replica_groups=mesh['cp'=8,'tp'=4] {'cp'}, dimensions={0}, use_global_device_ids=true | all-gather | bytes 9216 | tf_op jit(solution)/shard_map/all_gather | solution.py:138
  48.2 0.5 multiply_cosine_fusion
  48.7 36.1 %all-gather.4.cloned.1.call-done = bf16[256,4096]{1,0:T(8,128)(2,1)} async-done(((bf16[256,1024]{1,0:T(8,128)(2,1)}), bf16[256,4096]{1,0:T(8,128)(2,1)}) %all-gather.4.cloned.1.call-update) | async-done | bytes 2097168 | tf_op jit(solution)/shard_map/all_gather | solution.py:88
  84.8 2.4 %convolution_bitcast_fusion.2 = f32[256,1,128]{0,2,1:T(8,128)S(1)} fusion(bf16[256,4096]{1,0:T(8,128)(2,1)} %all-gather.4.cloned.1.call-done, bf16[4096,128]{1,0:T(8,128)(2,1)S(1)} %copy-done), kind=kOutput, calls=%fused_computation.34 | convolution fusion | flops 268435456 | bytes 3276800 | tf_op jit(solution)/shard_map/dot_general | solution.py:90
  87.3 0.3 fusion.30
  87.6 6.3 %convolution_bitcast_fusion.1 = f32[32,8,8,128]{3,1,2,0:T(8,128)S(1)} fusion(bf16[256,4096]{1,0:T(8,128)(2,1)} %all-gather.4.cloned.1.call-done, bf16[4096,1024]{1,0:T(8,128)(2,1)} %param.10), kind=kOutput, calls=%fused_computation.33 | convolution fusion | flops 2147483648 | bytes 11534336 | tf_op jit(solution)/shard_map/dot_general | solution.py:90
  94.2 0.5 fusion.23
  94.7 0.3 maximum_bitcast_fusion
  95.0 0.9 copy.41
  95.9 10.9 %all-gather = bf16[2048,1,128]{0,2,1:T(8,128)(2,1)S(1)} all-gather(bf16[256,1,128]{0,2,1:T(8,128)(2,1)S(1)} %pad_maximum_fusion), channel_id=2, replica_groups=mesh['cp'=8,'tp'=4] {'cp'}, dimensions={0}, use_global_device_ids=true | all-gather | bytes 589824 | tf_op jit(solution)/shard_map/all_gather | solution.py:136
  106.7 0.7 convolution_convert_fusion.1
  107.4 10.0 %all_gather.15 = bf16[2048,128]{1,0:T(8,128)(2,1)S(1)} all-gather(bf16[256,128]{1,0:T(8,128)(2,1)S(1)} %convolution_convert_fusion.1), channel_id=1, replica_groups=mesh['cp'=8,'tp'=4] {'cp'}, dimensions={0}, use_global_device_ids=true | all-gather | bytes 589824 | tf_op jit(solution)/shard_map/all_gather | solution.py:137
  117.4 28.0 %while.18 = (s32[]{:T(128)}, f32[1,2048]{1,0:T(1,128)S(1)}, f32[1,2048]{1,0:T(1,128)S(1)}, f32[1,2048,128]{2,1,0:T(8,128)S(1)}, s32[256]{0:T(256)S(1)}, /*index=...) while((s32[]{:T(128)}, f32[1,2048]{1,0:T(1,128)S(1)}, ...), condition=%wide.region_8.9_spmd.clone, body=%wide.region_4.8_spmd.clone.sunk | while | flops 551702784 | bytes 22166840 | solution.py:151
  118.0 0.5 tile.22
  118.4 0.6 copy.49
  119.1 2.0 fusion.53
  121.1 1.2 fusion.55
  122.4 2.0 %fusion.57 = f32[1,2048,128]{2,1,0:T(8,128)S(1)} fusion(pred[2048,512]{0,1:T(8,128)(4,1)S(1)} %bitcast.98, f32[512,2048]{1,0:T(8,128)S(1)} %get-tuple-element.403, f32[2048]{0:T(1024)S(1)} %bitcast.102, f32[1,2048,128]{2,1,0:T(8,128)S(1)} %get-tuple-element.424, f32[2048]{0:T(1024)S(1)} %bitcast.111, pred[]{:T(512)S(6)} %compare.3, ...), kind=kOutput, calls=%fused_computation.8.clone.1 | convolution fusion | flops 274464768 | bytes 7487493 | tf_op jit(solution)/shard_map/while/body/eval_jaxpr/khs,ksd->khd/dot_general | solution.py:123
  125.0 0.5 tile.22
  125.5 0.6 copy.49
  126.1 2.0 fusion.53
  128.1 1.2 fusion.55
  129.4 2.1 %fusion.57 = f32[1,2048,128]{2,1,0:T(8,128)S(1)} fusion(pred[2048,512]{0,1:T(8,128)(4,1)S(1)} %bitcast.98, f32[512,2048]{1,0:T(8,128)S(1)} %get-tuple-element.403, f32[2048]{0:T(1024)S(1)} %bitcast.102, f32[1,2048,128]{2,1,0:T(8,128)S(1)} %get-tuple-element.424, f32[2048]{0:T(1024)S(1)} %bitcast.111, pred[]{:T(512)S(6)} %compare.3, ...), kind=kOutput, calls=%fused_computation.8.clone.1 | convolution fusion | flops 274464768 | bytes 7487493 | tf_op jit(solution)/shard_map/while/body/eval_jaxpr/khs,ksd->khd/dot_general | solution.py:123
  132.0 0.5 tile.22
  132.5 0.6 copy.49
  133.1 2.0 fusion.53
  135.1 1.2 fusion.55
  136.4 2.0 %fusion.57 = f32[1,2048,128]{2,1,0:T(8,128)S(1)} fusion(pred[2048,512]{0,1:T(8,128)(4,1)S(1)} %bitcast.98, f32[512,2048]{1,0:T(8,128)S(1)} %get-tuple-element.403, f32[2048]{0:T(1024)S(1)} %bitcast.102, f32[1,2048,128]{2,1,0:T(8,128)S(1)} %get-tuple-element.424, f32[2048]{0:T(1024)S(1)} %bitcast.111, pred[]{:T(512)S(6)} %compare.3, ...), kind=kOutput, calls=%fused_computation.8.clone.1 | convolution fusion | flops 274464768 | bytes 7487493 | tf_op jit(solution)/shard_map/while/body/eval_jaxpr/khs,ksd->khd/dot_general | solution.py:123
  139.0 0.5 tile.22
  139.5 0.6 copy.49
  140.1 2.0 fusion.53
  142.1 1.2 fusion.55
  143.4 2.1 %fusion.57 = f32[1,2048,128]{2,1,0:T(8,128)S(1)} fusion(pred[2048,512]{0,1:T(8,128)(4,1)S(1)} %bitcast.98, f32[512,2048]{1,0:T(8,128)S(1)} %get-tuple-element.403, f32[2048]{0:T(1024)S(1)} %bitcast.102, f32[1,2048,128]{2,1,0:T(8,128)S(1)} %get-tuple-element.424, f32[2048]{0:T(1024)S(1)} %bitcast.111, pred[]{:T(512)S(6)} %compare.3, ...), kind=kOutput, calls=%fused_computation.8.clone.1 | convolution fusion | flops 274464768 | bytes 7487493 | tf_op jit(solution)/shard_map/while/body/eval_jaxpr/khs,ksd->khd/dot_general | solution.py:123
  145.5 0.3 divide_convert_fusion
  145.8 0.2 copy.43
  146.1 7.1 %convolution_convert_fusion = bf16[256,4096]{1,0:T(8,128)(2,1)} fusion(bf16[256,1024]{0,1:T(8,128)(2,1)S(1)} %bitcast.103, bf16[1024,4096]{1,0:T(8,128)(2,1)} %param.13), kind=kOutput, calls=%fused_computation.32 | convolution fusion | flops 2148532224 | bytes 11010048 | tf_op jit(solution)/shard_map/dot_general | solution.py:160
  153.2 41.7 %reduce-scatter.2.cloned.1.call-done = bf16[256,1024]{1,0:T(8,128)(2,1)} async-done(((bf16[256,4096]{1,0:T(8,128)(2,1)}), bf16[256,1024]{1,0:T(8,128)(2,1)}) %reduce-scatter.2.cloned.1.call-update) | async-done | bytes 524304 | tf_op jit(solution)/shard_map/reduce_scatter | solution.py:161
  (64 shorter events, 3.7 us)
Async XLA Ops:
  6.5 78.3 %copy-start = (bf16[4096,128]{1,0:T(8,128)(2,1)S(1)}, bf16[4096,128]{1,0:T(8,128)(2,1)}, u32[]{:S(2)}) copy-start(bf16[4096,128]{1,0:T(8,128)(2,1)} %param.11) | copy-start | bytes 3145732
  9.2 14.9 %all-to-all-start = ((bf16[2,8,16384]{2,0,1:T(2,128)(2,1)}), bf16[2,8,16384]{2,0,1:T(2,128)(2,1)S(1)}, u32[]{:S(2)}, u32[]{:S(2)}) async-start(bf16[2,8,16384]{2,0,1:T(2,128)(2,1)} %copy.37), calls=%async_computation | async-start | bytes 1048576 | tf_op jit(solution)/shard_map/all_to_all | solution.py:78
  14.4 70.4 %all-gather.4.cloned.1.call-start = ((), (), s32[]{:S(2)}) async-start(), calls=%async_computation.3 | async-start | bytes 2621440 | tf_op jit(solution)/shard_map/all_gather | solution.py:88
  24.4 15.4 %copy-start.3 = (s32[9]{0:T(128)S(1)}, s32[9]{0:T(128)}, u32[]{:S(2)}) copy-start(s32[9]{0:T(128)} %param.14) | copy-start | bytes 112
  39.7 155.2 %reduce-scatter.2.cloned.1.call-start = ((), (), s32[]{:S(2)}) async-start(), calls=%async_computation.4 | async-start | bytes 2621440 | tf_op jit(solution)/shard_map/reduce_scatter | solution.py:161
  93.9 12.8 %copy-start.1 = (bf16[256,4096]{1,0:T(8,128)(2,1)S(1)}, bf16[256,4096]{1,0:T(8,128)(2,1)}, u32[]{:S(2)}) copy-start(bf16[256,4096]{1,0:T(8,128)(2,1)} %all-gather.4.cloned.1.call-done) | copy-start | bytes 6291460
  93.9 12.8 %copy-start.2 = (bf16[4096,128]{1,0:T(8,128)(2,1)S(1)}, bf16[4096,128]{1,0:T(8,128)(2,1)}, u32[]{:S(2)}) copy-start(bf16[4096,128]{1,0:T(8,128)(2,1)} %param.12) | copy-start | bytes 3145732
Sparse Core Ops, SparseCore 0:
  39.8 45.0 all-gather.3
  153.3 41.4 reduce-scatter.1
where the time goes:
time: 202 us
  waiting for transfers between devices  85.5 us (42%)
  blocking collectives  40.9 us (20%)
  matrix products  32.6 us (16%)
  between operations  13.6 us (7%)
  local copies, waits for them, and re-layouts  11.8 us (6%)
  other arithmetic  11.7 us (6%)
  starting transfers between devices  5.28 us (3%)
    reduce_scatter x1, waiting for transfers between devices, output_rows(): lax.psum_scatter(head_terms.astype(jnp.bfloat16), 'tp', scatter_dimension...  41.7 us
    all_gather x1, waiting for transfers between devices, project(): portion = lax.all_gather(local_rows, 'tp', axis=1, tiled=True)  36.1 us
    all_to_all x1, blocking collectives, relayout(): lax.all_to_all(outgoing, 'cp', split_axis=1, concat_axis=1, tiled=True)  12.1 us
    all_gather x1, blocking collectives, attend(): key_part = lax.all_gather(key_rows, 'cp', axis=0, tiled=True)  10.9 us
    all_gather x1, blocking collectives, attend(): value_part = lax.all_gather(value_rows, 'cp', axis=0, tiled=True)  9.99 us
    dot_general x3, matrix products, project(): jnp.dot(portion, weight, preferred_element_type=jnp.float32)  9.46 us
    dot_general x4, matrix products, update(): jnp.einsum('khs,ksd->khd', weights.astype(jnp.bfloat16), per_head_values,...  8.2 us
    all_gather x1, blocking collectives, attend(): token_part = lax.all_gather(key_tokens, 'cp', axis=0, tiled=True)  7.96 us
  transfers between devices with their start and end apart: 3, of which 3 were waited for; matrix products, arithmetic and copies ran while one was open for 1% of the time, Pallas kernels for 0%

commit v1 on v0

--- a/solution.py
+++ b/solution.py
@@ -1,8 +1,11 @@
+import functools
 import math
 
 import jax
 import jax.numpy as jnp
 from jax import lax
+from jax.experimental import pallas as pl
+from jax.experimental.pallas import tpu as pltpu
 from jax.sharding import PartitionSpec as P
 
 HEAD_WIDTH = 128
@@ -161,7 +164,504 @@
     return lax.psum_scatter(head_terms.astype(jnp.bfloat16), "tp", scatter_dimension=1, tiled=True)
 
 
-def local(
+MESH = pl.DeviceIdType.MESH
+WINDOW = 512
+
+
+def dot(a, b):
+    return jnp.dot(a, b, preferred_element_type=jnp.float32)
+
+
+def turn(raw, cosine, sine):
+    half = raw.shape[1] // 2
+    swapped = jnp.concatenate([raw[:, half:], raw[:, :half]], axis=1)
+    return (raw * cosine + swapped * sine).astype(jnp.bfloat16)
+
+
+def greet(n_cp, n_tp):
+    c, z = lax.axis_index("cp"), lax.axis_index("tp")
+    barrier = pltpu.get_barrier_semaphore()
+    for t in range(1, n_cp):
+        peer = lax.rem(c + t, n_cp)
+        pl.semaphore_signal(barrier, inc=1, device_id={"cp": peer}, device_id_type=MESH)
+    for t in range(1, n_tp):
+        peer = lax.rem(z + t, n_tp)
+        pl.semaphore_signal(barrier, inc=1, device_id={"tp": peer}, device_id_type=MESH)
+    pl.semaphore_wait(barrier, n_cp + n_tp - 2)
+
+
+def project_kernel(
+    n_cp, n_tp,
+    hidden, wq_hbm, wk_hbm, wv_hbm, cosine, sine,
+    q_out, kv_out,
+    rows, wq, wkv, acc_q, acc_kv, kv_own, kv_all,
+    w_sem, own_sem, s_send, s_recv, r_send, l_send, z_recv, k_send, k_recv, d_send, d_recv, kown_sem,
+):
+    c, z = lax.axis_index("cp"), lax.axis_index("tp")
+    per = hidden.shape[0]
+    width = hidden.shape[3]
+    weights = (
+        pltpu.make_async_copy(wq_hbm, wq, w_sem.at[0]),
+        pltpu.make_async_copy(wk_hbm, wkv.at[:, pl.ds(0, HEAD_WIDTH)], w_sem.at[1]),
+        pltpu.make_async_copy(wv_hbm, wkv.at[:, pl.ds(HEAD_WIDTH, HEAD_WIDTH)], w_sem.at[2]),
+    )
+    own = pltpu.make_async_copy(hidden.at[:, c], rows.at[z, pl.ds(c * per, per)], own_sem)
+    own.start()
+    greet(n_cp, n_tp)
+
+    def spread(t):
+        peer = lax.rem(c + t, n_cp)
+        return pltpu.make_async_remote_copy(
+            src_ref=hidden.at[:, peer], dst_ref=rows.at[z, pl.ds(c * per, per)],
+            send_sem=s_send.at[t], recv_sem=s_recv.at[t],
+            device_id={"cp": peer}, device_id_type=MESH,
+        )
+
+    def along(origin, t, step):
+        source = lax.rem(c - t + n_cp, n_cp)
+        piece = rows.at[origin, pl.ds(source * per, per)]
+        sems = r_send if step > 0 else l_send
+        return pltpu.make_async_remote_copy(
+            src_ref=piece, dst_ref=piece,
+            send_sem=sems.at[origin, t], recv_sem=z_recv.at[origin, t],
+            device_id={"tp": lax.rem(z + step + n_tp, n_tp)}, device_id_type=MESH,
+        )
+
+    def multiply(origin, first):
+        block = rows[origin].reshape(-1, width)
+        span = pl.ds(pl.multiple_of(origin * width, width), width)
+        kv_term = dot(block, wkv[span, :])
+        q_term = dot(block, wq[span, :])
+        if first:
+            acc_kv[...] = kv_term
+            acc_q[...] = q_term
+        else:
+            acc_kv[...] += kv_term
+            acc_q[...] += q_term
+
+    for t in range(1, n_cp):
+        spread(t).start()
+    for copy in weights:
+        copy.start()
+    for t in range(n_cp):
+        if t == 0:
+            own.wait()
+        else:
+            spread(t).wait_recv()
+
+        @pl.when(z < n_tp - 1)
+        def _():
+            along(z, t, 1).start()
+
+        @pl.when(z > 0)
+        def _():
+            along(z, t, -1).start()
+
+    for copy in weights:
+        copy.wait()
+    multiply(z, True)
+
+    @pl.loop(1, n_tp)
+    def _(s):
+        for t in range(n_cp):
+            @pl.when(z - s >= 0)
+            def _():
+                along(z - s, t, 1).wait_recv()
+
+                @pl.when(z < n_tp - 1)
+                def _():
+                    along(z - s, t, 1).start()
+
+            @pl.when(z + s < n_tp)
+            def _():
+                along(z + s, t, -1).wait_recv()
+
+                @pl.when(z > 0)
+                def _():
+                    along(z + s, t, -1).start()
+
+        @pl.when(z - s >= 0)
+        def _():
+            multiply(z - s, False)
+
+        @pl.when(z + s < n_tp)
+        def _():
+            multiply(z + s, False)
+
+    key = turn(acc_kv[:, :HEAD_WIDTH], cosine[...], sine[...])
+    value = acc_kv[:, HEAD_WIDTH:].astype(jnp.bfloat16)
+    kv_own[...] = jnp.concatenate([key, value], axis=1).reshape(kv_own.shape)
+    chips = n_cp // 2
+    partner = c + 1 - 2 * lax.rem(c, 2)
+    mine = pltpu.make_async_copy(kv_own, kv_all.at[:, c], kown_sem)
+
+    def across(i):
+        return pltpu.make_async_remote_copy(
+            src_ref=kv_own, dst_ref=kv_all.at[:, c],
+            send_sem=k_send.at[i], recv_sem=k_recv.at[i],
+            device_id={"cp": lax.rem(c + 2 * i, n_cp)}, device_id_type=MESH,
+        )
+
+    def handed(i):
+        source = lax.rem(c - 2 * i + n_cp, n_cp)
+        return pltpu.make_async_remote_copy(
+            src_ref=kv_own if i == 0 else kv_all.at[:, source], dst_ref=kv_all.at[:, source],
+            send_sem=d_send.at[i], recv_sem=d_recv.at[i],
+            device_id={"cp": partner}, device_id_type=MESH,
+        )
+
+    for i in range(1, chips):
+        across(i).start()
+    handed(0).start()
+    mine.start()
+    for h in range(q_out.shape[1] // HEAD_WIDTH):
+        cols = slice(h * HEAD_WIDTH, (h + 1) * HEAD_WIDTH)
+        q_out[:, cols] = turn(acc_q[:, cols], cosine[...], sine[...])
+    for i in range(1, chips):
+        across(i).wait_recv()
+        handed(i).start()
+    mine.wait()
+    for i in range(chips):
+        handed(i).wait_recv()
+    kv_out[...] = kv_all[...]
+    for t in range(1, n_cp):
+        spread(t).wait_send()
+    for t in range(n_cp):
+        for o in range(n_tp):
+            @pl.when((z < n_tp - 1) & (o <= z))
+            def _():
+                along(o, t, 1).wait_send()
+
+            @pl.when((z > 0) & (o >= z))
+            def _():
+                along(o, t, -1).wait_send()
+    for i in range(1, chips):
+        across(i).wait_send()
+    for i in range(chips):
+        handed(i).wait_send()
+
+
+def project_call(hidden, wq, wk, wv, cosine, sine, n_cp, n_tp):
+    rows, width = hidden.shape
+    per = rows // BLOCK
+    share = BLOCK // n_cp
+    blocks = per * n_cp
+    pieces = hidden.reshape(per, n_cp, share, width)
+    bf, dma = jnp.bfloat16, pltpu.SemaphoreType.DMA
+    vmem = pl.BlockSpec(memory_space=pltpu.VMEM)
+    hbm = pl.BlockSpec(memory_space=pl.ANY)
+    flops = 2 * rows * wq.shape[0] * (wq.shape[1] + 2 * HEAD_WIDTH)
+    return pl.pallas_call(
+        functools.partial(project_kernel, n_cp, n_tp),
+        out_shape=(
+            jax.ShapeDtypeStruct((rows, wq.shape[1]), bf),
+            jax.ShapeDtypeStruct((blocks, n_cp, share, 2 * HEAD_WIDTH), bf),
+        ),
+        in_specs=[vmem, hbm, hbm, hbm, vmem, vmem],
+        out_specs=(vmem, vmem),
+        scratch_shapes=[
+            pltpu.VMEM((n_tp, blocks, share, width), bf),
+            pltpu.VMEM(wq.shape, bf),
+            pltpu.VMEM((wq.shape[0], 2 * HEAD_WIDTH), bf),
+            pltpu.VMEM((rows, wq.shape[1]), jnp.float32),
+            pltpu.VMEM((rows, 2 * HEAD_WIDTH), jnp.float32),
+            pltpu.VMEM((blocks, share, 2 * HEAD_WIDTH), bf),
+            pltpu.VMEM((blocks, n_cp, share, 2 * HEAD_WIDTH), bf),
+            dma((3,)), dma, dma((n_cp,)), dma((n_cp,)),
+            dma((n_tp, n_cp)), dma((n_tp, n_cp)), dma((n_tp, n_cp)),
+            dma((n_cp,)), dma((n_cp,)), dma((n_cp,)), dma((n_cp,)), dma,
+        ],
+        compiler_params=pltpu.CompilerParams(
+            collective_id=1, has_side_effects=True, vmem_limit_bytes=48 << 20
+        ),
+        cost_estimate=pl.CostEstimate(flops=flops, bytes_accessed=12 << 20, transcendentals=0),
+    )(pieces, wq, wk, wv, cosine, sine)
+
+
+def attend_kernel(first_key, where, q_ref, kv_ref, start_ref, token_ref, out_ref, *, heads):
+    blocks, share = q_ref.shape[0], q_ref.shape[1]
+    scale = 1.0 / math.sqrt(HEAD_WIDTH)
+    keys = kv_ref.shape[0]
+    window = min(WINDOW, keys)
+
+    def stack(tile):
+        return jnp.concatenate(
+            [tile[:, h * HEAD_WIDTH : (h + 1) * HEAD_WIDTH] for h in range(heads)], axis=0
+        )
+
+    def scored(q, begin, stop, start, token):
+        span = pl.ds(pl.multiple_of(begin, BLOCK), window)
+        key = kv_ref[span, :HEAD_WIDTH]
+        value = kv_ref[span, HEAD_WIDTH:]
+        score = lax.dot_general(
+            q, key, (((1,), (1,)), ((), ())), preferred_element_type=jnp.float32
+        ) * scale
+        index = begin + lax.broadcasted_iota(jnp.int32, score.shape, 1)
+        allowed = (index >= start) & (index <= token) & (index < stop)
+        return jnp.where(allowed, score, masked_score), allowed, value
+
+    def one(b):
+        q = stack(q_ref[b])
+        start = jnp.tile(start_ref[b], (heads, 1))[:, :1]
+        token = jnp.tile(token_ref[b], (heads, 1))[:, :1]
+        stop = (b + 1) * BLOCK
+        begin = jnp.maximum(stop - window, 0)
+        score, allowed, value = scored(q, begin, stop, start, token)
+        top = jnp.max(score, axis=1, keepdims=True)
+        weight = jnp.where(allowed, jnp.exp(score - top), 0.0)
+        total = jnp.sum(weight, axis=1, keepdims=True)
+        out = dot(weight.astype(jnp.bfloat16), value)
+        low = first_key[b]
+
+        def more(carry):
+            stop, top, total, out = carry
+            begin = jnp.maximum(stop - window, 0)
+            score, allowed, value = scored(q, begin, stop, start, token)
+            new_top = jnp.maximum(top, jnp.max(score, axis=1, keepdims=True))
+            weight = jnp.where(allowed, jnp.exp(score - new_top), 0.0)
+            factor = jnp.exp(top - new_top)
+            total = total * factor + jnp.sum(weight, axis=1, keepdims=True)
+            out = out * factor + dot(weight.astype(jnp.bfloat16), value)
+            return begin, new_top, total, out
+
+        return low, more, (begin, top, total, out)
+
+    group = 4
+
+    @pl.loop(0, blocks // group)
+    def _(g):
+        firsts = [one(g * group + i) for i in range(group)]
+        for i, (low, more, carry) in enumerate(firsts):
+            _, _, total, out = lax.while_loop(lambda state: state[0] > low, more, carry)
+            out = (out / total).astype(jnp.bfloat16)
+            tile = jnp.concatenate(
+                [out[h * share : (h + 1) * share] for h in range(heads)], axis=1
+            )
+            out_ref[where[g * group + i]] = tile
+
+
+def attend_call(q, kv, first_key, where, start, token, n_cp):
+    rows, width = q.shape
+    share = BLOCK // n_cp
+    blocks = rows // share
+    vmem = pl.BlockSpec(memory_space=pltpu.VMEM)
+    smem = pl.BlockSpec(memory_space=pltpu.SMEM)
+    lanes = lambda a: jnp.broadcast_to(a.reshape(blocks, share, 1), (blocks, share, HEAD_WIDTH))
+    return pl.pallas_call(
+        functools.partial(attend_kernel, heads=width // HEAD_WIDTH),
+        out_shape=jax.ShapeDtypeStruct((blocks, share, width), jnp.bfloat16),
+        in_specs=[smem, smem, vmem, vmem, vmem, vmem],
+        out_specs=vmem,
+        compiler_params=pltpu.CompilerParams(vmem_limit_bytes=32 << 20),
+    )(
+        first_key, where, q.reshape(blocks, share, width),
+        kv.reshape(-1, 2 * HEAD_WIDTH), lanes(start), lanes(token),
+    )
+
+
+def output_kernel(
+    n_cp, n_tp, heads, wo_hbm, out_ref,
+    wo, part, from_left, from_right, to_right, to_left, done, landed,
+    w_sem, r_send, l_send, r_recv, l_recv, a_send, a_recv,
+):
+    c, z = lax.axis_index("cp"), lax.axis_index("tp")
+    per = out_ref.shape[0]
+    share, width = heads.shape[1], out_ref.shape[3]
+
+    def weight(o):
+        cols = pl.ds(pl.multiple_of(o * width, width), width)
+        return pltpu.make_async_copy(wo_hbm.at[:, cols], wo.at[o], w_sem.at[o])
+
+    for s in range(n_tp - 1, -1, -1):
+        @pl.when(z + s < n_tp)
+        def _():
+            weight(z + s).start()
+
+        if s > 0:
+            @pl.when(z - s >= 0)
+            def _():
+                weight(z - s).start()
+
+    greet(n_cp, n_tp)
+
+    def piece(t):
+        return pl.ds(lax.rem(c + t, n_cp) * per, per)
+
+    def rightward(o, t):
+        return pltpu.make_async_remote_copy(
+            src_ref=to_right.at[o, piece(t)], dst_ref=from_left.at[o, piece(t)],
+            send_sem=r_send.at[o, t], recv_sem=r_recv.at[o, t],
+            device_id={"tp": lax.rem(z + 1, n_tp)}, device_id_type=MESH,
+        )
+
+    def leftward(o, t):
+        return pltpu.make_async_remote_copy(
+            src_ref=to_left.at[o, piece(t)], dst_ref=from_right.at[o, piece(t)],
+            send_sem=l_send.at[o, t], recv_sem=l_recv.at[o, t],
+            device_id={"tp": lax.rem(z + n_tp - 1, n_tp)}, device_id_type=MESH,
+        )
+
+    def final(t):
+        peer = lax.rem(c + t, n_cp)
+        return pltpu.make_async_remote_copy(
+            src_ref=done.at[piece(t)], dst_ref=landed.at[:, c],
+            send_sem=a_send.at[t], recv_sem=a_recv.at[t],
+            device_id={"cp": peer}, device_id_type=MESH,
+        )
+
+    def term(o):
+        weight(o).wait()
+        block = heads[...].reshape(-1, heads.shape[2])
+        return dot(block, wo[o]).reshape(part.shape[1:])
+
+    order = list(range(1, n_cp)) + [0]
+
+    @pl.loop(0, n_tp - 1)
+    def _(i):
+        s = n_tp - 1 - i
+
+        @pl.when(z + s < n_tp)
+        def _():
+            product = term(z + s)
+
+            @pl.when(z == 0)
+            def _():
+                to_right[z + s] = product.astype(jnp.bfloat16)
+                for t in order:
+                    rightward(z + s, t).start()
+
+            @pl.when(z > 0)
+            def _():
+                part[z + s] = product
+
+        @pl.when(z - s >= 0)
+        def _():
+            product = term(z - s)
+
+            @pl.when(z == n_tp - 1)
+            def _():
+                to_left[z - s] = product.astype(jnp.bfloat16)
+                for t in order:
+                    leftward(z - s, t).start()
+
+            @pl.when(z < n_tp - 1)
+            def _():
+                part[z - s] = product
+
+    part[z] = term(z)
+
+    @pl.loop(0, n_tp - 1)
+    def _(i):
+        s = n_tp - 1 - i
+        for t in order:
+            @pl.when((z + s < n_tp) & (z > 0))
+            def _():
+                rightward(z + s, t).wait_recv()
+                total = part[z + s, piece(t)] + from_left[z + s, piece(t)].astype(jnp.float32)
+                to_right[z + s, piece(t)] = total.astype(jnp.bfloat16)
+                rightward(z + s, t).start()
+
+            @pl.when((z - s >= 0) & (z < n_tp - 1))
+            def _():
+                leftward(z - s, t).wait_recv()
+                total = part[z - s, piece(t)] + from_right[z - s, piece(t)].astype(jnp.float32)
+                to_left[z - s, piece(t)] = total.astype(jnp.bfloat16)
+                leftward(z - s, t).start()
+
+    for t in order:
+        @pl.when(z > 0)
+        def _():
+            rightward(z, t).wait_recv()
+            part[z, piece(t)] += from_left[z, piece(t)].astype(jnp.float32)
+
+        @pl.when(z < n_tp - 1)
+        def _():
+            leftward(z, t).wait_recv()
+            part[z, piece(t)] += from_right[z, piece(t)].astype(jnp.float32)
+
+        done[piece(t)] = part[z, piece(t)].astype(jnp.bfloat16)
+        if t > 0:
+            final(t).start()
+
+    for t in range(1, n_cp):
+        final(t).wait_recv()
+        source = lax.rem(c - t + n_cp, n_cp)
+        out_ref[:, pl.ds(source, 1)] = landed[:, pl.ds(source, 1)]
+    out_ref[:, pl.ds(c, 1)] = done[piece(0)][:, None]
+    for t in range(1, n_cp):
+        final(t).wait_send()
+    for t in range(n_cp):
+        for o in range(n_tp):
+            @pl.when(o > z)
+            def _():
+                rightward(o, t).wait_send()
+
+            @pl.when(o < z)
+            def _():
+                leftward(o, t).wait_send()
+
+
+def output_call(heads, wo, n_cp, n_tp):
+    blocks, share, depth = heads.shape
+    width = wo.shape[1] // n_tp
+    per = blocks // n_cp
+    bf, dma = jnp.bfloat16, pltpu.SemaphoreType.DMA
+    vmem = pl.BlockSpec(memory_space=pltpu.VMEM)
+    slab = (n_tp, blocks, share, width)
+    out = pl.pallas_call(
+        functools.partial(output_kernel, n_cp, n_tp),
+        out_shape=jax.ShapeDtypeStruct((per, n_cp, share, width), bf),
+        in_specs=[vmem, pl.BlockSpec(memory_space=pl.ANY)],
+        out_specs=vmem,
+        scratch_shapes=[
+            pltpu.VMEM((n_tp, depth, width), bf),
+            pltpu.VMEM(slab, jnp.float32),
+            pltpu.VMEM(slab, bf), pltpu.VMEM(slab, bf), pltpu.VMEM(slab, bf), pltpu.VMEM(slab, bf),
+            pltpu.VMEM(slab[1:], bf),
+            pltpu.VMEM((per, n_cp, share, width), bf),
+            dma((n_tp,)), dma((n_tp, n_cp)), dma((n_tp, n_cp)), dma((n_tp, n_cp)), dma((n_tp, n_cp)),
+            dma((n_cp,)), dma((n_cp,)),
+        ],
+        compiler_params=pltpu.CompilerParams(
+            collective_id=2, has_side_effects=True, vmem_limit_bytes=48 << 20
+        ),
+        cost_estimate=pl.CostEstimate(
+            flops=2 * blocks * share * depth * wo.shape[1], bytes_accessed=12 << 20, transcendentals=0
+        ),
+    )(heads, wo)
+    return out.reshape(per * n_cp * share, width)
+
+
+def local_fused(
+    hidden, query_weight, key_matrix, value_matrix, output_weight, document_bounds, block_owner
+):
+    n_cp, n_tp = lax.axis_size("cp"), lax.axis_size("tp")
+    c = lax.axis_index("cp")
+    per = hidden.shape[0] // BLOCK
+    share = BLOCK // n_cp
+    blocks = block_owner.shape[0]
+    index = jnp.arange(blocks, dtype=jnp.int32)
+    tokens = (
+        index[:, None] * BLOCK + c * share + jnp.arange(share, dtype=jnp.int32)[None, :]
+    ).reshape(-1)
+    position = position_of(tokens, document_bounds)
+    angles = position.astype(jnp.float32)[:, None] * rope_inverse(HEAD_WIDTH)[None, :]
+    cosine, sine = jnp.cos(angles), jnp.sin(angles)
+    cosine = jnp.concatenate([cosine, cosine], axis=1)
+    sine = jnp.concatenate([-sine, sine], axis=1)
+    starts = tokens - position
+    first_key = jnp.min(starts.reshape(blocks, share), axis=1)
+    same_owner = block_owner[:, None] == block_owner[None, :]
+    rank = jnp.sum((same_owner & (index[None, :] < index[:, None])).astype(jnp.int32), axis=1)
+    slot = block_owner * per + rank
+    q, kv = project_call(
+        hidden, query_weight, key_matrix, value_matrix, cosine, sine, n_cp, n_tp
+    )
+    heads = attend_call(q, kv, first_key, slot, starts, tokens, n_cp)
+    return output_call(heads, output_weight, n_cp, n_tp)
+
+
+def local_plain(
     hidden, query_weight, key_matrix, value_matrix, output_weight, document_bounds, block_owner
 ):
     cp_index = lax.axis_index("cp")
@@ -185,6 +685,8 @@
 
 
 def solution(mesh):
+    shares = BLOCK // mesh.shape["cp"]
+    local = local_fused if shares % 16 == 0 else local_plain
     placed = (P("cp", "tp"), P(None, "tp"), P(None, "tp"), P(None, "tp"), P("tp", None), P(), P())
     return jax.shard_map(
         local, mesh=mesh, in_specs=placed, out_specs=P("cp", "tp"), check_vma=False

time: 202 us -> 109 us (0.54)
  the two profiles are of different devices: /device:TPU:0 before, /device:TPU:9 now
where the time goes in v1:
time: 109 us
  Pallas kernels  101 us (93%)
  local copies, waits for them, and re-layouts  4.62 us (4%)
  other arithmetic  3.21 us (3%)
    pallas_call x1, Pallas kernels, output_call(): pl.pallas_call(functools.partial(output_kernel, n_cp, n_tp), out_shape=ja...  52.7 us
    pallas_call x1, Pallas kernels, project_call(): pl.pallas_call(functools.partial(project_kernel, n_cp, n_tp), out_shape=(...  40.8 us
    pallas_call x1, Pallas kernels, attend_call(): pl.pallas_call(functools.partial(attend_kernel, heads=width // HEAD_WIDTH...  7.41 us
    unnamed x7, local copies, waits for them, and re-layouts  4.28 us

profile of v1, /device:TPU:9, one launch (start us, length us, event | category | flops | bytes accessed | tf_op | source)
XLA Modules:
  0.0 108.9 jit_solution(15271736236810689905)
XLA Ops:
  0.0 0.9 convert_reduce_fusion
  0.9 0.7 multiply_add_fusion.where
  1.6 0.1 iota_add_fusion
  1.7 0.1 add.61
  1.8 0.7 select_reduce_fusion
  2.5 0.1 reshape.96
  2.6 0.1 reduce_min.9.first_key
  2.7 0.1 broadcast_in_dim.15.start_ref
  2.8 0.1 broadcast_in_dim.16.token_ref
  2.9 0.5 fusion
  3.5 0.1 pad_maximum_fusion
  3.6 0.0 copy-start
  3.6 1.2 %copy-done = bf16[4096,128]{1,0:T(8,128)(2,1)S(1)} copy-done((bf16[4096,128]{1,0:T(8,128)(2,1)S(1)}, bf16[4096,128]{1,0:T(8,128)(2,1)}, u32[]{:S(2)}) %copy-start) | copy-done | bytes 1048600
  4.8 0.0 copy-start.1
  4.8 1.2 %copy-done.1 = bf16[4096,128]{1,0:T(8,128)(2,1)S(1)} copy-done((bf16[4096,128]{1,0:T(8,128)(2,1)S(1)}, bf16[4096,128]{1,0:T(8,128)(2,1)}, u32[]{:S(2)}) %copy-start.1) | copy-done | bytes 1048600
  6.0 0.0 copy-start.2
  6.1 1.0 copy-done.2
  7.1 40.8 %shard_map.73 = (bf16[256,1024]{1,0:T(8,128)(2,1)S(1)}, bf16[16,8,16,256]{3,2,1,0:T(8,128)(2,1)S(1)}) custom-call(bf16[2,8,16,1024]{3,2,1,0:T(8,128)(2,1)S(1)} %bitcast.7, bf16[4096,1024]{1,0:T(8,128)(2,1)} %wq_hbm.1, bf16[4096,128]{1,0:T(8,128)(2,1)S(1)} %copy-done, bf16[4096,128]{1,0:T(8,128)(2,1)S(1)} %copy-done.1, ...), custom_call_target="tpu_custom_call" | custom-call | flops 2684354560 | bytes 12582912 | tf_op jit(solution)/shard_map/pallas_call | solution.py:354
  47.9 7.4 %shard_map.74.heads = bf16[16,16,1024]{2,1,0:T(8,128)(2,1)S(1)} custom-call(s32[16]{0:T(128)S(1)} %reduce_min.9.first_key, s32[16]{0:T(128)S(1)} %multiply_add_fusion.where, bf16[16,16,1024]{2,1,0:T(8,128)(2,1)S(1)} %bitcast.8, bf16[2048,256]{1,0:T(8,128)(2,1)S(1)} %bitcast.6, s32[16,16,128]{2,1,0:T(8,128)S(1)} %broadcast_in_dim.15.start_ref, ...), custom_call_target="tpu_custom_call" | custom-call | tf_op jit(solution)/shard_map/pallas_call | solution.py:450
  55.3 52.7 %shard_map.75 = bf16[2,8,16,1024]{3,2,1,0:T(8,128)(2,1)S(1)} custom-call(bf16[16,16,1024]{2,1,0:T(8,128)(2,1)S(1)} %shard_map.74.heads, bf16[1024,4096]{1,0:T(8,128)(2,1)} %wo_hbm.1), custom_call_target="tpu_custom_call" | custom-call | flops 2147483648 | bytes 12582912 | tf_op jit(solution)/shard_map/pallas_call | solution.py:611
  108.1 0.8 copy.9
  (3 shorter events, 0.0 us)
Async XLA Ops:
  3.6 1.2 %copy-start = (bf16[4096,128]{1,0:T(8,128)(2,1)S(1)}, bf16[4096,128]{1,0:T(8,128)(2,1)}, u32[]{:S(2)}) copy-start(bf16[4096,128]{1,0:T(8,128)(2,1)} %wk_hbm.1) | copy-start | bytes 3145732
  4.8 1.2 %copy-start.1 = (bf16[4096,128]{1,0:T(8,128)(2,1)S(1)}, bf16[4096,128]{1,0:T(8,128)(2,1)}, u32[]{:S(2)}) copy-start(bf16[4096,128]{1,0:T(8,128)(2,1)} %wv_hbm.1) | copy-start | bytes 3145732
  6.0 1.0 copy-start.2

commit v2 on v1

--- a/solution.py
+++ b/solution.py
@@ -190,12 +190,24 @@
     pl.semaphore_wait(barrier, n_cp + n_tp - 2)
 
 
+def row_tokens(bounds, blocks, share, offset):
+    shape = (blocks, share, HEAD_WIDTH)
+    token = (
+        lax.broadcasted_iota(jnp.int32, shape, 0) * BLOCK
+        + lax.broadcasted_iota(jnp.int32, shape, 1) + offset
+    )
+    start = jnp.zeros_like(token)
+    for i in range(bounds.shape[0] - 1):
+        start = jnp.where(token >= bounds[i], bounds[i], start)
+    return token, start
+
+
 def project_kernel(
     n_cp, n_tp,
-    hidden, wq_hbm, wk_hbm, wv_hbm, cosine, sine,
+    bounds, hidden, wq_hbm, wk_hbm, wv_hbm, inverse,
     q_out, kv_out,
-    rows, wq, wkv, acc_q, acc_kv, kv_own, kv_all,
-    w_sem, own_sem, s_send, s_recv, r_send, l_send, z_recv, k_send, k_recv, d_send, d_recv, kown_sem,
+    rows, wq, wkv, acc_q, acc_kv, kv_own, kv_all, cosine, sine,
+    w_sem, own_sem, s_send, s_recv, r_send, l_send, z_recv, k_send, k_recv, d_send, d_recv,
 ):
     c, z = lax.axis_index("cp"), lax.axis_index("tp")
     per = hidden.shape[0]
@@ -257,11 +269,17 @@
         def _():
             along(z, t, -1).start()
 
+    blocks, share = kv_own.shape[0], kv_own.shape[1]
+    token, start = row_tokens(bounds, blocks, share, c * share)
+    angle = (token - start).astype(jnp.float32).reshape(-1, HEAD_WIDTH) * inverse[...]
+    cosine[...] = jnp.cos(angle)
+    lane = lax.broadcasted_iota(jnp.int32, angle.shape, 1)
+    sine[...] = jnp.where(lane < HEAD_WIDTH // 2, -1.0, 1.0) * jnp.sin(angle)
     for copy in weights:
         copy.wait()
     multiply(z, True)
 
-    @pl.loop(1, n_tp)
+    @pl.loop(1, n_tp - 1)
     def _(s):
         for t in range(n_cp):
             @pl.when(z - s >= 0)
@@ -288,41 +306,84 @@
         def _():
             multiply(z + s, False)
 
-    key = turn(acc_kv[:, :HEAD_WIDTH], cosine[...], sine[...])
-    value = acc_kv[:, HEAD_WIDTH:].astype(jnp.bfloat16)
-    kv_own[...] = jnp.concatenate([key, value], axis=1).reshape(kv_own.shape)
     chips = n_cp // 2
     partner = c + 1 - 2 * lax.rem(c, 2)
-    mine = pltpu.make_async_copy(kv_own, kv_all.at[:, c], kown_sem)
-
-    def across(i):
+    count = per * share
+    far = n_tp - 1 - z
+    last = (z == 0) | (z == n_tp - 1)
+    far_span = pl.ds(pl.multiple_of(far * width, width), width)
+
+    def part_of(t):
+        return lax.rem(c - t + n_cp, n_cp)
+
+    def across(i, t):
+        span = pl.ds(part_of(t) * per, per)
         return pltpu.make_async_remote_copy(
-            src_ref=kv_own, dst_ref=kv_all.at[:, c],
-            send_sem=k_send.at[i], recv_sem=k_recv.at[i],
+            src_ref=kv_own.at[span], dst_ref=kv_all.at[span, c],
+            send_sem=k_send.at[i, t], recv_sem=k_recv.at[i, t],
             device_id={"cp": lax.rem(c + 2 * i, n_cp)}, device_id_type=MESH,
         )
 
-    def handed(i):
+    def arrived(i, t):
         source = lax.rem(c - 2 * i + n_cp, n_cp)
+        span = pl.ds(lax.rem(source - t + n_cp, n_cp) * per, per)
+        landed = kv_all.at[span, source]
         return pltpu.make_async_remote_copy(
-            src_ref=kv_own if i == 0 else kv_all.at[:, source], dst_ref=kv_all.at[:, source],
-            send_sem=d_send.at[i], recv_sem=d_recv.at[i],
+            src_ref=landed, dst_ref=landed,
+            send_sem=d_send.at[i, t], recv_sem=d_recv.at[i, t],
             device_id={"cp": partner}, device_id_type=MESH,
         )
 
-    for i in range(1, chips):
-        across(i).start()
-    handed(0).start()
-    mine.start()
-    for h in range(q_out.shape[1] // HEAD_WIDTH):
-        cols = slice(h * HEAD_WIDTH, (h + 1) * HEAD_WIDTH)
-        q_out[:, cols] = turn(acc_q[:, cols], cosine[...], sine[...])
-    for i in range(1, chips):
-        across(i).wait_recv()
-        handed(i).start()
-    mine.wait()
-    for i in range(chips):
-        handed(i).wait_recv()
+    def handed(t):
+        span = pl.ds(part_of(t) * per, per)
+        return pltpu.make_async_remote_copy(
+            src_ref=kv_own.at[span], dst_ref=kv_all.at[span, c],
+            send_sem=d_send.at[0, t], recv_sem=d_recv.at[0, t],
+            device_id={"cp": partner}, device_id_type=MESH,
+        )
+
+    @pl.loop(0, n_cp)
+    def _(t):
+        span = pl.ds(part_of(t) * per, per)
+        lines = pl.ds(pl.multiple_of(part_of(t) * count, count), count)
+
+        @pl.when(last)
+        def _():
+            along(far, t, 1).wait_recv()
+            block = rows[far, span].reshape(count, width)
+            acc_kv[lines, :] += dot(block, wkv[far_span, :])
+
+        cos_t, sin_t = cosine[lines, :], sine[lines, :]
+        key = turn(acc_kv[lines, :HEAD_WIDTH], cos_t, sin_t)
+        value = acc_kv[lines, HEAD_WIDTH:].astype(jnp.bfloat16)
+        tile = jnp.concatenate([key, value], axis=1).reshape(per, share, 2 * HEAD_WIDTH)
+        kv_own[span] = tile
+        kv_all[span, pl.ds(c, 1)] = tile[:, None]
+        for i in range(1, chips):
+            across(i, t).start()
+        handed(t).start()
+
+        @pl.when(last)
+        def _():
+            block = rows[far, span].reshape(count, width)
+            acc_q[lines, :] += dot(block, wq[far_span, :])
+
+        for h in range(q_out.shape[1] // HEAD_WIDTH):
+            cols = slice(h * HEAD_WIDTH, (h + 1) * HEAD_WIDTH)
+            q_out[lines, cols] = turn(acc_q[lines, cols], cos_t, sin_t)
+
+    @pl.loop(0, n_cp)
+    def _(t):
+        for i in range(1, chips):
+            across(i, t).wait_recv()
+            arrived(i, t).start()
+
+    @pl.loop(0, n_cp)
+    def _(t):
+        handed(t).wait_recv()
+        for i in range(1, chips):
+            arrived(i, t).wait_recv()
+
     kv_out[...] = kv_all[...]
     for t in range(1, n_cp):
         spread(t).wait_send()
@@ -335,13 +396,16 @@
             @pl.when((z > 0) & (o >= z))
             def _():
                 along(o, t, -1).wait_send()
-    for i in range(1, chips):
-        across(i).wait_send()
-    for i in range(chips):
-        handed(i).wait_send()
-
-
-def project_call(hidden, wq, wk, wv, cosine, sine, n_cp, n_tp):
+
+    @pl.loop(0, n_cp)
+    def _(t):
+        handed(t).wait_send()
+        for i in range(1, chips):
+            across(i, t).wait_send()
+            arrived(i, t).wait_send()
+
+
+def project_call(bounds, hidden, wq, wk, wv, inverse, n_cp, n_tp):
     rows, width = hidden.shape
     per = rows // BLOCK
     share = BLOCK // n_cp
@@ -349,7 +413,8 @@
     pieces = hidden.reshape(per, n_cp, share, width)
     bf, dma = jnp.bfloat16, pltpu.SemaphoreType.DMA
     vmem = pl.BlockSpec(memory_space=pltpu.VMEM)
-    hbm = pl.BlockSpec(memory_space=pl.ANY)
+    hbm = pl.BlockSpec(memory_space=pltpu.HBM)
+    smem = pl.BlockSpec(memory_space=pltpu.SMEM)
     flops = 2 * rows * wq.shape[0] * (wq.shape[1] + 2 * HEAD_WIDTH)
     return pl.pallas_call(
         functools.partial(project_kernel, n_cp, n_tp),
@@ -357,7 +422,7 @@
             jax.ShapeDtypeStruct((rows, wq.shape[1]), bf),
             jax.ShapeDtypeStruct((blocks, n_cp, share, 2 * HEAD_WIDTH), bf),
         ),
-        in_specs=[vmem, hbm, hbm, hbm, vmem, vmem],
+        in_specs=[smem, hbm, hbm, hbm, hbm, vmem],
         out_specs=(vmem, vmem),
         scratch_shapes=[
             pltpu.VMEM((n_tp, blocks, share, width), bf),
@@ -367,22 +432,35 @@
             pltpu.VMEM((rows, 2 * HEAD_WIDTH), jnp.float32),
             pltpu.VMEM((blocks, share, 2 * HEAD_WIDTH), bf),
             pltpu.VMEM((blocks, n_cp, share, 2 * HEAD_WIDTH), bf),
+            pltpu.VMEM((rows, HEAD_WIDTH), jnp.float32),
+            pltpu.VMEM((rows, HEAD_WIDTH), jnp.float32),
             dma((3,)), dma, dma((n_cp,)), dma((n_cp,)),
             dma((n_tp, n_cp)), dma((n_tp, n_cp)), dma((n_tp, n_cp)),
-            dma((n_cp,)), dma((n_cp,)), dma((n_cp,)), dma((n_cp,)), dma,
+            dma((n_cp // 2, n_cp)), dma((n_cp // 2, n_cp)),
+            dma((n_cp // 2, n_cp)), dma((n_cp // 2, n_cp)),
         ],
         compiler_params=pltpu.CompilerParams(
             collective_id=1, has_side_effects=True, vmem_limit_bytes=48 << 20
         ),
         cost_estimate=pl.CostEstimate(flops=flops, bytes_accessed=12 << 20, transcendentals=0),
-    )(pieces, wq, wk, wv, cosine, sine)
-
-
-def attend_kernel(first_key, where, q_ref, kv_ref, start_ref, token_ref, out_ref, *, heads):
+    )(bounds, pieces, wq, wk, wv, inverse)
+
+
+def attend_kernel(bounds, owner, q_ref, kv_ref, out_ref, starts, tokens, where, *, heads, per):
     blocks, share = q_ref.shape[0], q_ref.shape[1]
-    scale = 1.0 / math.sqrt(HEAD_WIDTH)
+    offset = lax.axis_index("cp") * share
+    factor_of = math.log2(math.e) / math.sqrt(HEAD_WIDTH)
     keys = kv_ref.shape[0]
     window = min(WINDOW, keys)
+    token_all, start_all = row_tokens(bounds, blocks, share, offset)
+    tokens[...] = token_all
+    starts[...] = start_all
+    for d in range(blocks // per):
+        where[blocks + d] = d * per
+    for b in range(blocks):
+        slot = where[blocks + owner[b]]
+        where[b] = slot
+        where[blocks + owner[b]] = slot + 1
 
     def stack(tile):
         return jnp.concatenate(
@@ -395,31 +473,34 @@
         value = kv_ref[span, HEAD_WIDTH:]
         score = lax.dot_general(
             q, key, (((1,), (1,)), ((), ())), preferred_element_type=jnp.float32
-        ) * scale
+        )
         index = begin + lax.broadcasted_iota(jnp.int32, score.shape, 1)
-        allowed = (index >= start) & (index <= token) & (index < stop)
-        return jnp.where(allowed, score, masked_score), allowed, value
+        allowed = (index >= start) & (index <= token)
+        if stop is not None:
+            allowed = allowed & (index < stop)
+        return jnp.where(allowed, score, masked_score), value
 
     def one(b):
         q = stack(q_ref[b])
-        start = jnp.tile(start_ref[b], (heads, 1))[:, :1]
-        token = jnp.tile(token_ref[b], (heads, 1))[:, :1]
-        stop = (b + 1) * BLOCK
-        begin = jnp.maximum(stop - window, 0)
-        score, allowed, value = scored(q, begin, stop, start, token)
+        start = jnp.tile(starts[b], (heads, 1))[:, :1]
+        token = jnp.tile(tokens[b], (heads, 1))[:, :1]
+        begin = jnp.maximum((b + 1) * BLOCK - window, 0)
+        score, value = scored(q, begin, None, start, token)
         top = jnp.max(score, axis=1, keepdims=True)
-        weight = jnp.where(allowed, jnp.exp(score - top), 0.0)
+        weight = jnp.exp2((score - top) * factor_of)
         total = jnp.sum(weight, axis=1, keepdims=True)
         out = dot(weight.astype(jnp.bfloat16), value)
-        low = first_key[b]
+        low = jnp.int32(0)
+        for i in range(bounds.shape[0] - 1):
+            low = jnp.where(b * BLOCK + offset >= bounds[i], bounds[i], low)
 
         def more(carry):
             stop, top, total, out = carry
             begin = jnp.maximum(stop - window, 0)
-            score, allowed, value = scored(q, begin, stop, start, token)
+            score, value = scored(q, begin, stop, start, token)
             new_top = jnp.maximum(top, jnp.max(score, axis=1, keepdims=True))
-            weight = jnp.where(allowed, jnp.exp(score - new_top), 0.0)
-            factor = jnp.exp(top - new_top)
+            weight = jnp.exp2((score - new_top) * factor_of)
+            factor = jnp.exp2((top - new_top) * factor_of)
             total = total * factor + jnp.sum(weight, axis=1, keepdims=True)
             out = out * factor + dot(weight.astype(jnp.bfloat16), value)
             return begin, new_top, total, out
@@ -440,23 +521,24 @@
             out_ref[where[g * group + i]] = tile
 
 
-def attend_call(q, kv, first_key, where, start, token, n_cp):
+def attend_call(bounds, owner, q, kv, n_cp):
     rows, width = q.shape
     share = BLOCK // n_cp
     blocks = rows // share
     vmem = pl.BlockSpec(memory_space=pltpu.VMEM)
     smem = pl.BlockSpec(memory_space=pltpu.SMEM)
-    lanes = lambda a: jnp.broadcast_to(a.reshape(blocks, share, 1), (blocks, share, HEAD_WIDTH))
     return pl.pallas_call(
-        functools.partial(attend_kernel, heads=width // HEAD_WIDTH),
+        functools.partial(attend_kernel, heads=width // HEAD_WIDTH, per=blocks // n_cp),
         out_shape=jax.ShapeDtypeStruct((blocks, share, width), jnp.bfloat16),
-        in_specs=[smem, smem, vmem, vmem, vmem, vmem],
+        in_specs=[smem, smem, vmem, vmem],
         out_specs=vmem,
+        scratch_shapes=[
+            pltpu.VMEM((blocks, share, HEAD_WIDTH), jnp.int32),
+            pltpu.VMEM((blocks, share, HEAD_WIDTH), jnp.int32),
+            pltpu.SMEM((blocks + n_cp,), jnp.int32),
+        ],
         compiler_params=pltpu.CompilerParams(vmem_limit_bytes=32 << 20),
-    )(
-        first_key, where, q.reshape(blocks, share, width),
-        kv.reshape(-1, 2 * HEAD_WIDTH), lanes(start), lanes(token),
-    )
+    )(bounds, owner, q.reshape(blocks, share, width), kv.reshape(-1, 2 * HEAD_WIDTH))
 
 
 def output_kernel(
@@ -611,7 +693,7 @@
     out = pl.pallas_call(
         functools.partial(output_kernel, n_cp, n_tp),
         out_shape=jax.ShapeDtypeStruct((per, n_cp, share, width), bf),
-        in_specs=[vmem, pl.BlockSpec(memory_space=pl.ANY)],
+        in_specs=[vmem, pl.BlockSpec(memory_space=pltpu.HBM)],
         out_specs=vmem,
         scratch_shapes=[
             pltpu.VMEM((n_tp, depth, width), bf),
@@ -636,28 +718,11 @@
     hidden, query_weight, key_matrix, value_matrix, output_weight, document_bounds, block_owner
 ):
     n_cp, n_tp = lax.axis_size("cp"), lax.axis_size("tp")
-    c = lax.axis_index("cp")
-    per = hidden.shape[0] // BLOCK
-    share = BLOCK // n_cp
-    blocks = block_owner.shape[0]
-    index = jnp.arange(blocks, dtype=jnp.int32)
-    tokens = (
-        index[:, None] * BLOCK + c * share + jnp.arange(share, dtype=jnp.int32)[None, :]
-    ).reshape(-1)
-    position = position_of(tokens, document_bounds)
-    angles = position.astype(jnp.float32)[:, None] * rope_inverse(HEAD_WIDTH)[None, :]
-    cosine, sine = jnp.cos(angles), jnp.sin(angles)
-    cosine = jnp.concatenate([cosine, cosine], axis=1)
-    sine = jnp.concatenate([-sine, sine], axis=1)
-    starts = tokens - position
-    first_key = jnp.min(starts.reshape(blocks, share), axis=1)
-    same_owner = block_owner[:, None] == block_owner[None, :]
-    rank = jnp.sum((same_owner & (index[None, :] < index[:, None])).astype(jnp.int32), axis=1)
-    slot = block_owner * per + rank
+    inverse = jnp.tile(rope_inverse(HEAD_WIDTH), 2)[None, :]
     q, kv = project_call(
-        hidden, query_weight, key_matrix, value_matrix, cosine, sine, n_cp, n_tp
-    )
-    heads = attend_call(q, kv, first_key, slot, starts, tokens, n_cp)
+        document_bounds, hidden, query_weight, key_matrix, value_matrix, inverse, n_cp, n_tp
+    )
+    heads = attend_call(document_bounds, block_owner, q, kv, n_cp)
     return output_call(heads, output_weight, n_cp, n_tp)
 
 

time: 109 us -> 102 us (0.936)
  Pallas kernels: 101 us -> 96 us
  other arithmetic: 3.21 us -> 0.02 us
    pallas_call x1, Pallas kernels: 52.7 us -> 47.6 us  [output_call(): pl.pallas_call(functools.partial(output_kernel, n_cp, n_tp), out_shape=ja...]
    pallas_call x1, Pallas kernels: 40.8 us -> 42.3 us  [project_call(): pl.pallas_call(functools.partial(project_kernel, n_cp, n_tp), out_shape=(...]
    pallas_call x1, Pallas kernels: 7.41 us -> 6.06 us  [attend_call(): pl.pallas_call(functools.partial(attend_kernel, heads=width // HEAD_WIDTH...]
    unnamed x7 -> x13, local copies, waits for them, and re-layouts: 4.28 us -> 4.95 us
where the time goes in v2:
time: 102 us; the launch traced here: 101 us
  Pallas kernels  96 us (94%)
  local copies, waits for them, and re-layouts  5.04 us (5%)
    pallas_call x1, Pallas kernels, output_call(): pl.pallas_call(functools.partial(output_kernel, n_cp, n_tp), out_shape=ja...  47.6 us
    pallas_call x1, Pallas kernels, project_call(): pl.pallas_call(functools.partial(project_kernel, n_cp, n_tp), out_shape=(...  42.3 us
    pallas_call x1, Pallas kernels, attend_call(): pl.pallas_call(functools.partial(attend_kernel, heads=width // HEAD_WIDTH...  6.06 us
    unnamed x13, local copies, waits for them, and re-layouts  4.95 us

profile of v2, /device:TPU:9, one launch (start us, length us, event | category | flops | bytes accessed | tf_op | source)
XLA Modules:
  0.0 101.1 jit_solution(15141212782689138113)
XLA Ops:
  0.0 0.0 copy-start.4
  0.0 0.0 copy-start.5
  0.0 0.1 broadcast_in_dim_tile.3.inverse
  0.1 0.0 copy-start
  0.1 1.2 %copy-done = bf16[4096,128]{1,0:T(8,128)(2,1)S(1)} copy-done((bf16[4096,128]{1,0:T(8,128)(2,1)S(1)}, bf16[4096,128]{1,0:T(8,128)(2,1)}, u32[]{:S(2)}) %copy-start) | copy-done | bytes 1048600
  1.3 0.0 copy-start.1
  1.3 1.2 %copy-done.1 = bf16[4096,128]{1,0:T(8,128)(2,1)S(1)} copy-done((bf16[4096,128]{1,0:T(8,128)(2,1)S(1)}, bf16[4096,128]{1,0:T(8,128)(2,1)}, u32[]{:S(2)}) %copy-start.1) | copy-done | bytes 1048600
  2.6 0.0 copy-start.2
  2.6 1.0 %copy-done.2 = bf16[256,1024]{1,0:T(8,128)(2,1)S(1)} copy-done((bf16[256,1024]{1,0:T(8,128)(2,1)S(1)}, bf16[256,1024]{1,0:T(8,128)(2,1)}, u32[]{:S(2)}) %copy-start.2) | copy-done | bytes 524312
  3.6 0.0 copy-start.3
  3.6 0.7 copy-done.3
  4.3 42.3 %shard_map.73 = (bf16[256,1024]{1,0:T(8,128)(2,1)S(1)}, bf16[16,8,16,256]{3,2,1,0:T(8,128)(2,1)S(1)}) custom-call(s32[9]{0:T(128)S(1)} %copy-done.3, bf16[2,8,16,1024]{3,2,1,0:T(8,128)(2,1)S(1)} %bitcast.6, bf16[4096,1024]{1,0:T(8,128)(2,1)} %wq_hbm.1, bf16[4096,128]{1,0:T(8,128)(2,1)S(1)} %copy-done, bf16[4096,128]{1,0:T(8,128)(2,1)S(1)} %copy-done.1, ...), custom_call_target="tpu_custom_call" | custom-call | flops 2684354560 | bytes 12582912 | tf_op jit(solution)/shard_map/pallas_call | solution.py:419
  46.6 0.0 copy-done.4
  46.6 0.0 copy-done.5
  46.6 6.1 %shard_map.74.heads = bf16[16,16,1024]{2,1,0:T(8,128)(2,1)S(1)} custom-call(s32[9]{0:T(128)S(1)} %copy-done.4, s32[16]{0:T(128)S(1)} %copy-done.5, bf16[16,16,1024]{2,1,0:T(8,128)(2,1)S(1)} %bitcast.7, bf16[2048,256]{1,0:T(8,128)(2,1)S(1)} %bitcast.5), custom_call_target="tpu_custom_call" | custom-call | tf_op jit(solution)/shard_map/pallas_call | solution.py:530
  52.7 47.6 %shard_map.75 = bf16[2,8,16,1024]{3,2,1,0:T(8,128)(2,1)S(1)} custom-call(bf16[16,16,1024]{2,1,0:T(8,128)(2,1)S(1)} %shard_map.74.heads, bf16[1024,4096]{1,0:T(8,128)(2,1)} %wo_hbm.1), custom_call_target="tpu_custom_call" | custom-call | flops 2147483648 | bytes 12582912 | tf_op jit(solution)/shard_map/pallas_call | solution.py:693
  100.3 0.8 copy.9
  (2 shorter events, 0.0 us)
Async XLA Ops:
  0.0 46.6 %copy-start.4 = (s32[9]{0:T(128)S(1)}, s32[9]{0:T(128)}, u32[]{:S(2)}) copy-start(s32[9]{0:T(128)} %bounds.3) | copy-start | bytes 112
  0.0 46.6 %copy-start.5 = (s32[16]{0:T(128)S(1)}, s32[16]{0:T(128)}, u32[]{:S(2)}) copy-start(s32[16]{0:T(128)} %owner.1) | copy-start | bytes 196
  0.1 1.2 %copy-start = (bf16[4096,128]{1,0:T(8,128)(2,1)S(1)}, bf16[4096,128]{1,0:T(8,128)(2,1)}, u32[]{:S(2)}) copy-start(bf16[4096,128]{1,0:T(8,128)(2,1)} %wk_hbm.1) | copy-start | bytes 3145732
  1.3 1.2 %copy-start.1 = (bf16[4096,128]{1,0:T(8,128)(2,1)S(1)}, bf16[4096,128]{1,0:T(8,128)(2,1)}, u32[]{:S(2)}) copy-start(bf16[4096,128]{1,0:T(8,128)(2,1)} %wv_hbm.1) | copy-start | bytes 3145732
  2.6 1.0 %copy-start.2 = (bf16[256,1024]{1,0:T(8,128)(2,1)S(1)}, bf16[256,1024]{1,0:T(8,128)(2,1)}, u32[]{:S(2)}) copy-start(bf16[256,1024]{1,0:T(8,128)(2,1)} %param.7) | copy-start | bytes 1572868
  3.6 0.7 copy-start.3
